TPU v7x, 32 devices: a whole 2x2x4 slice. The times are simulated.
32 devices in a mesh: grp: 4 (over y, x), cp: 8 (over z, core).
Axes of the slice: x: 2, y: 2, z: 4, core: 2. Of those that a mesh axis runs over, the one named last changes fastest.
Arguments:
- queries: bfloat16 [16384, 2048], P(('grp', 'cp')), parts along dimension 0, may hold values from -6 to 6
- keys: bfloat16 [16384, 1024], P(('grp', 'cp')), parts along dimension 0, may hold values from -8 to 8
- values: bfloat16 [16384, 1024], P(('grp', 'cp')), parts along dimension 0, may hold values from -6 to 6
- doc_lengths: int32 [128], P('grp'), parts along dimension 0, may hold values from 1 to 1024, 4096 in all
Outputs:
- attended: bfloat16 [16384, 2048], P(('grp', 'cp')), parts along dimension 0
There are 4 independent parts, one for each index of `grp`. A program takes and returns all parts, laid end to end along the dimension named above; each array names one. Nothing has to cross between parts.
Inputs may be any that keep to these rules, and one draw needn't show every extreme that they name: doc_lengths sums to 4096, and its largest entry is exactly 1024.
All inputs are finite; a program needn't handle non-finite values.
Results may differ from a plain program's by a relative error of at most 0.0031.
Values may be sent and summed in bfloat16 or wider, within the bound.
A program may use at most 64 MiB of HBM per device.

v0:
```python
import functools
import math

import jax
import jax.numpy as jnp
from jax import lax
from jax.experimental import pallas as pl
from jax.experimental.pallas import tpu as pltpu
from jax.sharding import PartitionSpec as P

HQ = 16
HK = 8
DH = 128
REACH = 2
GROUPS = HQ // HK
WIDTH = GROUPS * DH
TILE = 128
MASKED = -1e30

exponent_scale = 144.0 ** (-0.5) * math.log2(math.e)


LOG2E = math.log2(math.e)
SPLIT = HK // 2
MESH = pl.DeviceIdType.MESH


def kernel(
    shards,
    lengths_ref,
    queries_ref,
    keys_ref,
    values_ref,
    out_ref,
    held,
    query_held,
    out_held,
    query_back,
    slot,
    stat_out,
    stat_in,
    bias,
    back_bias,
    load_sem,
    query_sem,
    out_sem,
    core_send,
    core_recv,
    query_send,
    query_recv,
    slot_send,
    slot_recv,
    relay_send,
    relay_recv,
    stat_send,
    stat_recv,
):
    me = lax.axis_index("cp")
    core = lax.rem(me, 2)
    even = core == 0
    odd = core == 1
    partner = me + 1 - 2 * core
    rows = keys_ref.shape[0]
    docs = lengths_ref.shape[0]
    tiles = rows // TILE
    window = REACH * rows + TILE
    own = pl.ds(REACH * rows, rows)
    near = pl.ds(rows, rows)
    far = pl.ds(0, rows)
    has_prev = me >= 2
    has_next = me < shards - 2
    chip_begin = (me - core) * rows
    next_begin = chip_begin + 2 * rows

    def loads(head):
        lanes = pl.ds(pl.multiple_of(head * DH, DH), DH)
        return (
            pltpu.make_async_copy(keys_ref.at[:, lanes], held.at[head, 0, own], load_sem.at[head, 0]),
            pltpu.make_async_copy(values_ref.at[:, lanes], held.at[head, 1, own], load_sem.at[head, 1]),
        )

    def query_load(head):
        lanes = pl.ds(pl.multiple_of(head * WIDTH, WIDTH), WIDTH)
        return pltpu.make_async_copy(queries_ref.at[:, lanes], query_held.at[head], query_sem.at[head])

    def out_store(head):
        lanes = pl.ds(pl.multiple_of(head * WIDTH, WIDTH), WIDTH)
        return pltpu.make_async_copy(out_held.at[head], out_ref.at[:, lanes], out_sem.at[head])

    def remote(source, target, send, recv, device):
        return pltpu.make_async_remote_copy(
            src_ref=source,
            dst_ref=target,
            send_sem=send,
            recv_sem=recv,
            device_id={"cp": device},
            device_id_type=MESH,
        )

    def to_core(head, region):
        return remote(
            held.at[head, :, own], held.at[head, :, region], core_send.at[head], core_recv.at[head], partner
        )

    def query_to_prev(step, side):
        return remote(
            query_held.at[side * SPLIT + step],
            query_back.at[step],
            query_send.at[side * SPLIT + step],
            query_recv.at[step],
            me - 2 + side,
        )

    def slot_to_next(step, region):
        return remote(
            slot.at[step],
            held.at[core * SPLIT + step, :, region],
            slot_send.at[step],
            slot_recv.at[step],
            me + 2,
        )

    def relay(step, source, target):
        head = core * SPLIT + step
        return remote(
            held.at[head, :, source], held.at[head, :, target], relay_send.at[step], relay_recv.at[step], partner
        )

    def stat_to_next(step, head):
        return remote(
            stat_out.at[step], stat_in.at[head], stat_send.at[step], stat_recv.at[head], me + 2 - core
        )

    @pl.loop(0, SPLIT)
    def _(step):
        query_load(step).start()
        query_load(SPLIT + step).start()

    @pl.loop(0, HK)
    def _(head):
        for copy in loads(head):
            copy.start()

    barrier = pltpu.get_barrier_semaphore()

    def greet(device):
        pl.semaphore_signal(barrier, inc=1, device_id={"cp": device}, device_id_type=MESH)

    greet(partner)

    @pl.when(has_prev)
    def _():
        greet(me - 2)

        @pl.when(even)
        def _():
            greet(me - 1)

    @pl.when(has_next)
    def _():
        greet(me + 2)

        @pl.when(odd)
        def _():
            greet(me + 1)

    back_peers = jnp.where(has_prev, 2 - core, 0)
    next_peers = jnp.where(has_next, 1 + core, 0)
    pl.semaphore_wait(barrier, 1 + back_peers + next_peers)

    @pl.loop(0, SPLIT)
    def _(step):
        for side in range(2):
            query_load(side * SPLIT + step).wait()

            @pl.when(jnp.logical_and(even, has_prev))
            def _():
                query_to_prev(step, side).start()

    @pl.loop(0, HK)
    def _(head):
        for copy in loads(head):
            copy.wait()

        @pl.when(even)
        def _():
            to_core(head, near).start()

        @pl.when(jnp.logical_and(odd, head < SPLIT))
        def _():
            to_core(head, far).start()

    @pl.when(jnp.logical_not(has_prev))
    def _():
        @pl.when(even)
        def _():
            held[:, :, near, :] = jnp.zeros((HK, 2, rows, DH), held.dtype)
            stat_in[...] = jnp.full(stat_in.shape, MASKED, jnp.float32)

        @pl.when(odd)
        def _():
            held[:, :, far, :] = jnp.zeros((HK, 2, rows, DH), held.dtype)

    def doc_begins(positions):
        def next_doc(doc, state):
            end, begins = state
            end = end + lengths_ref[doc]
            return end, jnp.maximum(begins, jnp.where(positions >= end, end, 0))

        start = (jnp.int32(0), jnp.zeros(positions.shape, jnp.int32))
        return lax.fori_loop(0, docs, next_doc, start)[1]

    def sends_keys(boundary):
        positions = jnp.full((1, DH), boundary, jnp.int32)
        return boundary - doc_begins(positions) <= rows

    row_iota = lax.broadcasted_iota(jnp.int32, (TILE, 1), 0)
    floor = jnp.where(sends_keys(chip_begin), 0, chip_begin)[:, :1]
    for tile in range(tiles):
        query_pos = me * rows + tile * TILE + row_iota
        begins = jnp.maximum(doc_begins(query_pos), floor)
        first = jnp.where(even, (me - 1) * rows, (me - 2) * rows + tile * TILE)
        key_pos = first + lax.broadcasted_iota(jnp.int32, (TILE, window), 1)
        visible = (key_pos >= begins) & (key_pos <= query_pos)
        bias[pl.ds(tile * TILE, TILE), :] = jnp.where(visible, 0.0, MASKED)

    for tile in range(tiles):
        begins = doc_begins(next_begin + tile * TILE + row_iota)
        key_pos = chip_begin + lax.broadcasted_iota(jnp.int32, (TILE, 2 * rows), 1)
        back_bias[pl.ds(tile * TILE, TILE), :] = jnp.where(key_pos >= begins, 0.0, MASKED)

    next_keys = sends_keys(next_begin)
    diagonal = lax.broadcasted_iota(jnp.int32, (TILE, TILE), 0) == lax.broadcasted_iota(
        jnp.int32, (TILE, TILE), 1
    )

    def stack(queries):
        return jnp.concatenate([queries[:, g * DH : (g + 1) * DH] for g in range(GROUPS)], axis=0)

    def dot_keys(queries, keys):
        return lax.dot_general(
            queries, keys, (((1,), (1,)), ((), ())), preferred_element_type=jnp.float32
        )

    def softmax(scores, mask):
        scores = scores.reshape(GROUPS, TILE, scores.shape[-1]) * exponent_scale + mask[None]
        highest = jnp.max(scores, axis=-1, keepdims=True)
        weights = jnp.exp2(scores - highest)
        totals = jnp.sum(weights, axis=-1, keepdims=True)
        rounded = weights.astype(jnp.bfloat16).reshape(GROUPS * TILE, scores.shape[-1])
        return highest, totals, rounded

    def dot_values(weights, values):
        return jnp.dot(weights, values, preferred_element_type=jnp.float32)

    def attend_back(step):
        head = core * SPLIT + step
        older = pl.multiple_of((2 - core) * rows, TILE)
        newer = pl.multiple_of(2 * core * rows, TILE)
        newer_rows = pl.ds(newer, rows)
        for tile in range(tiles):
            span = pl.ds(tile * TILE, TILE)
            count = rows - tile * TILE
            older_rows = pl.ds(older + tile * TILE, count)
            queries = stack(query_back[step, span, :])
            scores = jnp.concatenate(
                [
                    dot_keys(queries, held[head, 0, older_rows, :]),
                    dot_keys(queries, held[head, 0, newer_rows, :]),
                ],
                axis=1,
            )
            highest, totals, weights = softmax(scores, back_bias[span, pl.ds(tile * TILE, count + rows)])
            mixed = dot_values(weights[:, :count], held[head, 1, older_rows, :]) + dot_values(
                weights[:, count:], held[head, 1, newer_rows, :]
            )
            mixed = mixed.reshape(GROUPS, TILE, DH) / totals
            level = highest + jnp.log(totals) * LOG2E
            sent = pl.ds(newer + tile * TILE, TILE)
            for g in range(GROUPS):
                kept = held[head, g, sent, :].astype(jnp.float32)
                slot[step, g, span, :] = jnp.where(next_keys, kept, mixed[g]).astype(jnp.bfloat16)
                row = jnp.sum(jnp.where(diagonal, level[g], 0.0), axis=0, keepdims=True)
                stat_out[step, pl.ds(tile * GROUPS + g, 1), :] = jnp.where(next_keys, MASKED, row)

    def attend_even(head):
        for tile in range(tiles):
            span = pl.ds(tile * TILE, TILE)
            count = rows + (tile + 1) * TILE
            keys = pl.ds(rows, count)
            scores = dot_keys(stack(query_held[head, span, :]), held[head, 0, keys, :])
            highest, totals, weights = softmax(scores, bias[span, pl.ds(0, count)])
            mixed = dot_values(weights, held[head, 1, keys, :]).reshape(GROUPS, TILE, DH)
            for g in range(GROUPS):
                row = stat_in[head, pl.ds(tile * GROUPS + g, 1), :]
                level = jnp.sum(jnp.where(diagonal, row, 0.0), axis=1, keepdims=True)
                top = jnp.maximum(highest[g], level)
                here = jnp.exp2(highest[g] - top)
                there = jnp.exp2(level - top)
                partial = held[head, g, pl.ds(rows + tile * TILE, TILE), :].astype(jnp.float32)
                both = (mixed[g] * here + partial * there) / (totals[g] * here + there)
                out_held[head, span, pl.ds(g * DH, DH)] = both.astype(jnp.bfloat16)

    def attend_odd(head):
        for tile in range(tiles):
            span = pl.ds(tile * TILE, TILE)
            keys = pl.ds(tile * TILE, window)
            scores = dot_keys(stack(query_held[head, span, :]), held[head, 0, keys, :])
            _, totals, weights = softmax(scores, bias[span, :])
            mixed = dot_values(weights, held[head, 1, keys, :]).reshape(GROUPS, TILE, DH)
            mixed = (mixed / totals).astype(jnp.bfloat16)
            for g in range(GROUPS):
                out_held[head, span, pl.ds(g * DH, DH)] = mixed[g]

    @pl.when(even)
    def _():
        @pl.loop(0, SPLIT)
        def _(head):
            to_core(head, far).wait_recv()

    @pl.when(odd)
    def _():
        @pl.loop(0, HK)
        def _(head):
            to_core(head, near).wait_recv()

    @pl.loop(0, SPLIT + 1)
    def _(turn):
        @pl.when(jnp.logical_and(has_next, turn < SPLIT))
        def _():
            query_to_prev(turn, 0).wait_recv()
            attend_back(turn)

            @pl.when(even)
            def _():
                slot_to_next(turn, near).start()

            @pl.when(odd)
            def _():
                slot_to_next(turn, far).start()

            stat_to_next(turn, core * SPLIT + turn).start()

        @pl.when(turn >= 1)
        def _():
            step = turn - 1

            @pl.when(has_prev)
            def _():
                slot_to_next(step, far).wait_recv()

                @pl.when(even)
                def _():
                    relay(step, near, far).start()

                @pl.when(odd)
                def _():
                    relay(step, far, near).start()

            @pl.loop(0, 2)
            def _(turn_side):
                side = lax.rem(core + turn_side, 2)
                head = side * SPLIT + step

                @pl.when(jnp.logical_and(has_prev, turn_side == 1))
                def _():
                    relay(step, near, far).wait_recv()

                @pl.when(even)
                def _():
                    @pl.when(has_prev)
                    def _():
                        stat_to_next(step, head).wait_recv()

                    attend_even(head)

                @pl.when(odd)
                def _():
                    attend_odd(head)

                out_store(head).start()

    @pl.loop(0, HK)
    def _(head):
        out_store(head).wait()

        @pl.when(jnp.logical_or(even, head < SPLIT))
        def _():
            to_core(head, near).wait_send()

    @pl.loop(0, SPLIT)
    def _(step):
        @pl.when(has_next)
        def _():
            slot_to_next(step, near).wait_send()
            stat_to_next(step, step).wait_send()

        @pl.when(has_prev)
        def _():
            relay(step, near, far).wait_send()

            @pl.when(even)
            def _():
                for side in range(2):
                    query_to_prev(step, side).wait_send()


def on_device(queries, keys, values, doc_lengths):
    rows = keys.shape[0]
    shards = lax.axis_size("cp")
    window = REACH * rows + TILE
    stats = rows // TILE * GROUPS
    dma = pltpu.SemaphoreType.DMA
    return pl.pallas_call(
        functools.partial(kernel, shards),
        out_shape=jax.ShapeDtypeStruct(queries.shape, queries.dtype),
        in_specs=[
            pl.BlockSpec(memory_space=pltpu.SMEM),
            pl.BlockSpec(memory_space=pl.ANY),
            pl.BlockSpec(memory_space=pl.ANY),
            pl.BlockSpec(memory_space=pl.ANY),
        ],
        out_specs=pl.BlockSpec(memory_space=pl.ANY),
        scratch_shapes=[
            pltpu.VMEM((HK, 2, (REACH + 1) * rows, DH), keys.dtype),
            pltpu.VMEM((HK, rows, WIDTH), queries.dtype),
            pltpu.VMEM((HK, rows, WIDTH), queries.dtype),
            pltpu.VMEM((SPLIT, rows, WIDTH), queries.dtype),
            pltpu.VMEM((SPLIT, 2, rows, DH), keys.dtype),
            pltpu.VMEM((SPLIT, stats, TILE), jnp.float32),
            pltpu.VMEM((HK, stats, TILE), jnp.float32),
            pltpu.VMEM((rows, window), jnp.float32),
            pltpu.VMEM((rows, REACH * rows), jnp.float32),
            dma((HK, 2)),
            dma((HK,)),
            dma((HK,)),
            dma((HK,)),
            dma((HK,)),
            dma((HK,)),
            dma((SPLIT,)),
            dma((SPLIT,)),
            dma((SPLIT,)),
            dma((SPLIT,)),
            dma((SPLIT,)),
            dma((SPLIT,)),
            dma((HK,)),
        ],
        compiler_params=pltpu.CompilerParams(
            collective_id=0, has_side_effects=True, vmem_limit_bytes=58 * 1024 * 1024
        ),
    )(doc_lengths, queries, keys, values)


def solution(mesh):
    return jax.shard_map(
        on_device,
        mesh=mesh,
        in_specs=(P(("grp", "cp"), None), P(("grp", "cp"), None), P(("grp", "cp"), None), P("grp")),
        out_specs=P(("grp", "cp"), None),
        check_vma=False,
    )
```

profile of v0, /device:TPU:1, one launch (start us, length us, event | category | flops | bytes accessed | tf_op | source)
XLA Modules:
  0.0 48.7 jit_solution(24301821344553946)
XLA Ops:
  0.0 45.6 %shard_map.46 = bf16[512,2048]{1,0:T(8,128)(2,1)} custom-call(s32[32]{0:T(128)} %lengths_ref.1, bf16[512,2048]{1,0:T(8,128)(2,1)} %queries_ref.1, bf16[512,1024]{1,0:T(8,128)(2,1)} %keys_ref.1, bf16[512,1024]{1,0:T(8,128)(2,1)} %values_ref.1), custom_call_target="tpu_custom_call" | custom-call | tf_op jit(solution)/shard_map/pallas_call | solution.py:414
  45.6 3.2 %copy.6 = bf16[512,2048]{1,0:T(8,128)(2,1)} copy(bf16[512,2048]{1,0:T(8,128)(2,1)} %shard_map.46) | data formatting | bytes 4194304
where the time goes:
time: 48.9 us; the launch traced here: 48.7 us
  Pallas kernels  45.6 us (93%)
  local copies, waits for them, and re-layouts  3.16 us (6%)
    pallas_call x1, Pallas kernels, on_device(): pl.pallas_call(functools.partial(kernel, shards), out_shape=jax.ShapeDtyp...  45.6 us
    unnamed x1, local copies, waits for them, and re-layouts  3.16 us

commit v1 on v0

v1 whole, which is shorter than its diff:
```python
import functools
import math

import jax
import jax.numpy as jnp
from jax import lax
from jax.experimental import pallas as pl
from jax.experimental.pallas import tpu as pltpu
from jax.sharding import PartitionSpec as P

HQ = 16
HK = 8
DH = 128
GROUPS = HQ // HK
WIDTH = GROUPS * DH
TILE = 128
STACK = GROUPS * TILE
MASKED = -1e30
SPLIT = HK // 2
MESH = pl.DeviceIdType.MESH

LOG2E = math.log2(math.e)
exponent_scale = 144.0 ** (-0.5) * LOG2E


def kernel(
    shards,
    lengths_ref,
    queries_ref,
    keys_ref,
    values_ref,
    out_ref,
    held,
    query_held,
    out_held,
    query_back,
    slot,
    stat_out,
    stat_in,
    bias,
    back_bias,
    lengths,
    mode,
    ones,
    part_mixed,
    part_total,
    part_high,
    lengths_sem,
    load_sem,
    query_sem,
    out_sem,
    core_send,
    core_recv,
    query_send,
    query_recv,
    slot_send,
    slot_recv,
    relay_send,
    relay_recv,
    stat_send,
    stat_recv,
):
    me = lax.axis_index("cp")
    core = lax.rem(me, 2)
    even = core == 0
    odd = core == 1
    partner = me + 1 - 2 * core
    rows = keys_ref.shape[0]
    docs = lengths_ref.shape[1]
    tiles = rows // TILE
    received = pl.ds(0, rows)
    own = pl.ds(pl.multiple_of((1 + core) * rows, rows), rows)
    has_prev = me >= 2
    has_next = me < shards - 2
    chip_begin = (me - core) * rows
    next_begin = chip_begin + 2 * rows

    def loads(head):
        lanes = pl.ds(pl.multiple_of(head * DH, DH), DH)
        return (
            pltpu.make_async_copy(keys_ref.at[:, lanes], held.at[head, 0, own], load_sem.at[head, 0]),
            pltpu.make_async_copy(values_ref.at[:, lanes], held.at[head, 1, own], load_sem.at[head, 1]),
        )

    def query_load(head):
        lanes = pl.ds(pl.multiple_of(head * WIDTH, WIDTH), WIDTH)
        return pltpu.make_async_copy(queries_ref.at[:, lanes], query_held.at[head], query_sem.at[head])

    def out_store(head):
        lanes = pl.ds(pl.multiple_of(head * WIDTH, WIDTH), WIDTH)
        return pltpu.make_async_copy(out_held.at[head], out_ref.at[:, lanes], out_sem.at[head])

    def remote(source, target, send, recv, device):
        return pltpu.make_async_remote_copy(
            src_ref=source,
            dst_ref=target,
            send_sem=send,
            recv_sem=recv,
            device_id={"cp": device},
            device_id_type=MESH,
        )

    def to_core(head):
        return remote(held.at[head, :, own], held.at[head, :, own], core_send.at[head], core_recv.at[head], partner)

    def from_core(head):
        other = pl.ds(pl.multiple_of((2 - core) * rows, rows), rows)
        return remote(held.at[head, :, other], held.at[head, :, other], core_send.at[head], core_recv.at[head], partner)

    def query_to_prev(step, side, tile):
        span = pl.ds(tile * TILE, TILE)
        return remote(
            query_held.at[side * SPLIT + step, span],
            query_back.at[step, span],
            query_send.at[side * SPLIT + step],
            query_recv.at[step, tile],
            me - 2 + side,
        )

    def query_sent(head):
        return remote(
            query_held.at[head], query_held.at[head], query_send.at[head], query_send.at[head], me - 2
        )

    def slot_to_next(step, span):
        return remote(
            slot.at[step, :, span],
            held.at[core * SPLIT + step, :, span],
            slot_send.at[step],
            slot_recv.at[step],
            me + 2,
        )

    def relay(step, side):
        head = side * SPLIT + step
        return remote(
            held.at[head, :, received], held.at[head, :, received], relay_send.at[step], relay_recv.at[step], partner
        )

    def stat_to_next(step, head):
        return remote(
            stat_out.at[step], stat_in.at[head], stat_send.at[step], stat_recv.at[head], me + 2 - core
        )

    barrier = pltpu.get_barrier_semaphore()

    def greet(device):
        pl.semaphore_signal(barrier, inc=1, device_id={"cp": device}, device_id_type=MESH)

    greet(partner)

    @pl.when(has_prev)
    def _():
        greet(me - 2)

        @pl.when(even)
        def _():
            greet(me - 1)

    @pl.when(has_next)
    def _():
        greet(me + 2)

        @pl.when(odd)
        def _():
            greet(me + 1)

    @pl.loop(0, SPLIT)
    def _(step):
        query_load(step).start()
        query_load(SPLIT + step).start()

    lengths_load = pltpu.make_async_copy(lengths_ref, lengths, lengths_sem)
    lengths_load.start()

    @pl.loop(0, HK)
    def _(head):
        for copy in loads(head):
            copy.start()

    back_peers = jnp.where(has_prev, 2 - core, 0)
    next_peers = jnp.where(has_next, 1 + core, 0)
    pl.semaphore_wait(barrier, 1 + back_peers + next_peers)

    @pl.loop(0, SPLIT)
    def _(step):
        query_load(step).wait()
        query_load(SPLIT + step).wait()

        @pl.when(jnp.logical_and(even, has_prev))
        def _():
            for tile in range(tiles):
                for side in range(2):
                    query_to_prev(step, side, tile).start()

    @pl.loop(0, HK)
    def _(head):
        for copy in loads(head):
            copy.wait()

        @pl.when(jnp.logical_or(even, head < SPLIT))
        def _():
            to_core(head).start()

    @pl.when(jnp.logical_not(has_prev))
    def _():
        held[:, :, received, :] = jnp.zeros((HK, 2, rows, DH), held.dtype)

        @pl.when(even)
        def _():
            stat_in[...] = jnp.full(stat_in.shape, MASKED, jnp.float32)

    ones[...] = jnp.ones(ones.shape, ones.dtype)

    lengths_load.wait()
    doc_row = lax.broadcasted_iota(jnp.int32, (docs, docs), 0)
    doc_lane = lax.broadcasted_iota(jnp.int32, (docs, docs), 1)
    length_row = lengths[...].astype(jnp.float32)
    length_column = jnp.sum(jnp.where(doc_row == doc_lane, length_row, 0.0), axis=1, keepdims=True)
    doc_ends = jnp.sum(jnp.where(doc_row <= doc_lane, length_column, 0.0), axis=0, keepdims=True)

    def doc_begins(positions):
        return jnp.max(jnp.where(positions >= doc_ends, doc_ends, 0.0), axis=1, keepdims=True)

    def boundary_begin(boundary):
        return doc_begins(jnp.full((8, 1), boundary, jnp.int32).astype(jnp.float32))

    def as_float(number):
        return jnp.full((1, 1), number, jnp.int32).astype(jnp.float32)

    row_iota = lax.broadcasted_iota(jnp.int32, (TILE, 1), 0)
    for tile in range(tiles):
        begins = doc_begins((next_begin + tile * TILE + row_iota).astype(jnp.float32))
        key_pos = (chip_begin + lax.broadcasted_iota(jnp.int32, (TILE, 2 * rows), 1)).astype(jnp.float32)
        back_bias[pl.ds(tile * TILE, TILE), :] = jnp.where(key_pos >= begins, 0.0, MASKED)

    next_wide = jnp.broadcast_to(boundary_begin(next_begin), (8, DH))
    mode[...] = next_wide

    begin_here = boundary_begin(chip_begin)[:1]
    here = as_float(chip_begin)
    floor = jnp.where(here - begin_here <= rows, 0.0, here)
    for tile in range(tiles):
        query_pos = (me * rows + tile * TILE + row_iota).astype(jnp.float32)
        begins = jnp.maximum(doc_begins(query_pos), floor)
        key_pos = (chip_begin - rows + lax.broadcasted_iota(jnp.int32, (TILE, 3 * rows), 1)).astype(jnp.float32)
        visible = (key_pos >= begins) & (key_pos <= query_pos)
        bias[pl.ds(tile * TILE, TILE), :] = jnp.where(visible, 0.0, MASKED)

    diagonal = lax.broadcasted_iota(jnp.int32, (TILE, TILE), 0) == lax.broadcasted_iota(
        jnp.int32, (TILE, TILE), 1
    )

    def stack(queries):
        return jnp.concatenate([queries[:, g * DH : (g + 1) * DH] for g in range(GROUPS)], axis=0)

    def raw_scores(queries, head, begin, count):
        keys = held[head, 0, pl.ds(begin, count), :]
        return lax.dot_general(
            stack(queries), keys, (((1,), (1,)), ((), ())), preferred_element_type=jnp.float32
        )

    def masked_scores(raw, mask):
        return raw.reshape(GROUPS, TILE, raw.shape[-1]) * exponent_scale + mask[None]

    def weigh(scores, highest, head, begin):
        count = scores.shape[-1]
        weights = jnp.exp2(scores - highest).astype(jnp.bfloat16).reshape(STACK, count)
        values = jnp.concatenate([held[head, 1, pl.ds(begin, count), :], ones[pl.ds(0, count), :]], axis=1)
        both = jnp.dot(weights, values, preferred_element_type=jnp.float32).reshape(GROUPS, TILE, 2 * DH)
        return both[:, :, :DH], both[:, :, DH:]

    def back_scores(step, head, tile):
        begin = rows + tile * TILE
        return raw_scores(query_back[step, pl.ds(tile * TILE, TILE), :], head, begin, 3 * rows - begin)

    def back_finish(step, head, tile, raw):
        begin = rows + tile * TILE
        span = pl.ds(tile * TILE, TILE)
        scores = masked_scores(raw, back_bias[span, pl.ds(tile * TILE, 2 * rows - tile * TILE)])
        highest = jnp.max(scores, axis=-1, keepdims=True)
        mixed, totals = weigh(scores, highest, head, begin)
        mixed = mixed * (1.0 / totals)
        level = highest + jnp.log2(totals)
        next_keys = as_float(next_begin) - mode[:1, :] <= rows
        for g in range(GROUPS):
            kept = held[head, g, pl.ds(2 * rows + tile * TILE, TILE), :].astype(jnp.float32)
            slot[step, g, span, :] = jnp.where(next_keys, kept, mixed[g]).astype(jnp.bfloat16)
            row = jnp.sum(jnp.where(diagonal, level[g], 0.0), axis=0, keepdims=True)
            stat_out[step, pl.ds(tile * GROUPS + g, 1), :] = jnp.where(next_keys, MASKED, row)

    def part_extent(side, tile):
        return rows, side * rows + (tile + 1) * TILE

    def part_scores(side, head, tile):
        return raw_scores(query_held[head, pl.ds(tile * TILE, TILE), :], head, *part_extent(side, tile))

    def part_finish(side, head, tile, raw):
        begin, count = part_extent(side, tile)
        span = pl.ds(tile * TILE, TILE)
        scores = masked_scores(raw, bias[span, pl.ds(begin, count)])
        highest = jnp.max(scores, axis=-1, keepdims=True)
        mixed, totals = weigh(scores, highest, head, begin)
        for g in range(GROUPS):
            part_mixed[head, g, span, :] = mixed[g]
            part_total[head, g, span, :] = totals[g]
            part_high[head, g, span, :] = jnp.broadcast_to(highest[g], (TILE, DH))

    def rest_extent(side, tile):
        begin = side * tile * TILE
        return begin, rows - begin

    def rest_scores(side, head, tile):
        return raw_scores(query_held[head, pl.ds(tile * TILE, TILE), :], head, *rest_extent(side, tile))

    def rest_finish(side, head, tile, raw):
        begin, count = rest_extent(side, tile)
        span = pl.ds(tile * TILE, TILE)
        scores = masked_scores(raw, bias[span, pl.ds(begin, count)])
        before = part_high[head, :, span, :]
        top = jnp.maximum(before, jnp.max(scores, axis=-1, keepdims=True))
        if side == 0:
            levels = []
            for g in range(GROUPS):
                row = stat_in[head, pl.ds(tile * GROUPS + g, 1), :]
                levels.append(jnp.sum(jnp.where(diagonal, row, 0.0), axis=1, keepdims=True))
            level = jnp.stack(levels)
            top = jnp.maximum(top, level)
        mixed, totals = weigh(scores, top[:, :, :1], head, begin)
        scale = jnp.exp2(before - top)
        mixed = mixed + part_mixed[head, :, span, :] * scale
        totals = totals + part_total[head, :, span, :] * scale
        if side == 0:
            there = jnp.exp2(level - top)
            mixed = mixed + held[head, :, span, :].astype(jnp.float32) * there
            totals = totals + there
        both = (mixed * (1.0 / totals)).astype(jnp.bfloat16)
        for g in range(GROUPS):
            out_held[head, span, pl.ds(g * DH, DH)] = both[g]

    def rest(side, head):
        raw = rest_scores(side, head, 0)
        for tile in range(tiles):
            later = rest_scores(side, head, tile + 1) if tile + 1 < tiles else None
            rest_finish(side, head, tile, raw)
            raw = later
        out_store(head).start()

    def wait_direct(side, step):
        @pl.when(has_prev)
        def _():
            slot_to_next(step, received).wait_recv()
            relay(step, side).start()
            if side == 0:
                stat_to_next(step, step).wait_recv()

    def wait_relayed(side, step):
        @pl.when(has_prev)
        def _():
            relay(step, 1 - side).wait_recv()
            if side == 0:
                stat_to_next(step, SPLIT + step).wait_recv()

    def run(side):
        @pl.loop(0, HK if side else SPLIT)
        def _(head):
            from_core(head).wait_recv()

        @pl.loop(0, SPLIT)
        def _(step):
            head = side * SPLIT + step
            for tile in range(tiles):
                @pl.when(has_next)
                def _():
                    query_to_prev(step, 0, tile).wait_recv()

                raw_back = back_scores(step, head, tile)
                raw_first = part_scores(side, step, tile)
                back_finish(step, head, tile, raw_back)

                @pl.when(has_next)
                def _():
                    slot_to_next(step, pl.ds(tile * TILE, TILE)).start()
                    if tile == tiles - 1:
                        stat_to_next(step, head).start()

                raw_second = part_scores(side, SPLIT + step, tile)
                part_finish(side, step, tile, raw_first)
                part_finish(side, SPLIT + step, tile, raw_second)

                if tile == tiles - 2:
                    @pl.when(step >= 1)
                    def _():
                        wait_direct(side, step - 1)

            @pl.when(step >= 1)
            def _():
                rest(side, side * SPLIT + step - 1)
                wait_relayed(side, step - 1)
                rest(side, (1 - side) * SPLIT + step - 1)

        wait_direct(side, SPLIT - 1)
        rest(side, side * SPLIT + SPLIT - 1)
        wait_relayed(side, SPLIT - 1)
        rest(side, (1 - side) * SPLIT + SPLIT - 1)

    @pl.when(even)
    def _():
        run(0)

    @pl.when(odd)
    def _():
        run(1)

    @pl.loop(0, HK)
    def _(head):
        out_store(head).wait()

        @pl.when(jnp.logical_or(even, head < SPLIT))
        def _():
            to_core(head).wait_send()

    @pl.loop(0, SPLIT)
    def _(step):
        @pl.when(has_next)
        def _():
            slot_to_next(step, received).wait_send()
            stat_to_next(step, step).wait_send()

        @pl.when(has_prev)
        def _():
            relay(step, core).wait_send()

            @pl.when(even)
            def _():
                for side in range(2):
                    query_sent(side * SPLIT + step).wait_send()


def on_device(queries, keys, values, doc_lengths):
    rows = keys.shape[0]
    docs = doc_lengths.shape[0]
    shards = lax.axis_size("cp")
    stats = rows // TILE * GROUPS
    dma = pltpu.SemaphoreType.DMA
    hbm = pl.BlockSpec(memory_space=pl.ANY)
    return pl.pallas_call(
        functools.partial(kernel, shards),
        out_shape=jax.ShapeDtypeStruct(queries.shape, queries.dtype),
        in_specs=[hbm] * 4,
        out_specs=hbm,
        scratch_shapes=[
            pltpu.VMEM((HK, 2, 3 * rows, DH), keys.dtype),
            pltpu.VMEM((HK, rows, WIDTH), queries.dtype),
            pltpu.VMEM((HK, rows, WIDTH), queries.dtype),
            pltpu.VMEM((SPLIT, rows, WIDTH), queries.dtype),
            pltpu.VMEM((SPLIT, 2, rows, DH), keys.dtype),
            pltpu.VMEM((SPLIT, stats, TILE), jnp.float32),
            pltpu.VMEM((HK, stats, TILE), jnp.float32),
            pltpu.VMEM((rows, 3 * rows), jnp.float32),
            pltpu.VMEM((rows, 2 * rows), jnp.float32),
            pltpu.VMEM((1, docs), jnp.int32),
            pltpu.VMEM((8, DH), jnp.float32),
            pltpu.VMEM((2 * rows, DH), keys.dtype),
            pltpu.VMEM((HK, GROUPS, rows, DH), jnp.float32),
            pltpu.VMEM((HK, GROUPS, rows, DH), jnp.float32),
            pltpu.VMEM((HK, GROUPS, rows, DH), jnp.float32),
            dma,
            dma((HK, 2)),
            dma((HK,)),
            dma((HK,)),
            dma((HK,)),
            dma((HK,)),
            dma((HK,)),
            dma((SPLIT, rows // TILE)),
            dma((SPLIT,)),
            dma((SPLIT,)),
            dma((SPLIT,)),
            dma((SPLIT,)),
            dma((SPLIT,)),
            dma((HK,)),
        ],
        compiler_params=pltpu.CompilerParams(
            collective_id=0, has_side_effects=True, vmem_limit_bytes=58 * 1024 * 1024
        ),
    )(doc_lengths.reshape(1, docs), queries, keys, values)


def solution(mesh):
    return jax.shard_map(
        on_device,
        mesh=mesh,
        in_specs=(P(("grp", "cp"), None), P(("grp", "cp"), None), P(("grp", "cp"), None), P("grp")),
        out_specs=P(("grp", "cp"), None),
        check_vma=False,
    )
```

time: 48.9 us -> 46.6 us (0.953)
  Pallas kernels: 45.6 us -> 43.3 us
    pallas_call x1, Pallas kernels: 45.6 us -> 43.3 us  [on_device(): pl.pallas_call(functools.partial(kernel, shards), out_shape=jax.ShapeDtyp...]
where the time goes in v1:
time: 46.6 us; the launch traced here: 46.5 us
  Pallas kernels  43.3 us (93%)
  local copies, waits for them, and re-layouts  3.16 us (7%)
    pallas_call x1, Pallas kernels, on_device(): pl.pallas_call(functools.partial(kernel, shards), out_shape=jax.ShapeDtyp...  43.3 us
    unnamed x1, local copies, waits for them, and re-layouts  3.16 us

profile of v1, /device:TPU:1, one launch (start us, length us, event | category | flops | bytes accessed | tf_op | source)
XLA Modules:
  0.0 46.5 jit_solution(12490299241253864401)
XLA Ops:
  0.0 43.3 %shard_map.46 = bf16[512,2048]{1,0:T(8,128)(2,1)} custom-call(s32[1,32]{1,0:T(1,128)} %bitcast.1, bf16[512,2048]{1,0:T(8,128)(2,1)} %queries_ref.1, bf16[512,1024]{1,0:T(8,128)(2,1)} %keys_ref.1, bf16[512,1024]{1,0:T(8,128)(2,1)} %values_ref.1), custom_call_target="tpu_custom_call" | custom-call | tf_op jit(solution)/shard_map/pallas_call | solution.py:447
  43.3 3.2 %copy.6 = bf16[512,2048]{1,0:T(8,128)(2,1)} copy(bf16[512,2048]{1,0:T(8,128)(2,1)} %shard_map.46) | data formatting | bytes 4194304

commit v2 on v1

--- a/solution.py
+++ b/solution.py
@@ -32,11 +32,14 @@
     out_ref,
     held,
     query_held,
-    out_held,
     query_back,
+    query_extra,
     slot,
+    slot_extra,
     stat_out,
     stat_in,
+    stat_extra_out,
+    stat_extra_in,
     bias,
     back_bias,
     lengths,
@@ -48,11 +51,14 @@
     lengths_sem,
     load_sem,
     query_sem,
-    out_sem,
     core_send,
     core_recv,
     query_send,
     query_recv,
+    extra_recv,
+    extra_send,
+    extra_stat_send,
+    extra_stat_recv,
     slot_send,
     slot_recv,
     relay_send,
@@ -82,13 +88,12 @@
             pltpu.make_async_copy(values_ref.at[:, lanes], held.at[head, 1, own], load_sem.at[head, 1]),
         )
 
+    def in_turn(turn):
+        return lax.rem(turn, 2) * SPLIT + turn // 2
+
     def query_load(head):
         lanes = pl.ds(pl.multiple_of(head * WIDTH, WIDTH), WIDTH)
         return pltpu.make_async_copy(queries_ref.at[:, lanes], query_held.at[head], query_sem.at[head])
-
-    def out_store(head):
-        lanes = pl.ds(pl.multiple_of(head * WIDTH, WIDTH), WIDTH)
-        return pltpu.make_async_copy(out_held.at[head], out_ref.at[:, lanes], out_sem.at[head])
 
     def remote(source, target, send, recv, device):
         return pltpu.make_async_remote_copy(
@@ -117,6 +122,33 @@
             me - 2 + side,
         )
 
+    def extra_query(step):
+        return remote(
+            query_held.at[SPLIT + step, pl.ds(0, TILE)],
+            query_extra.at[step],
+            query_send.at[SPLIT + step],
+            extra_recv.at[step],
+            me - 2,
+        )
+
+    def extra_slot(step):
+        return remote(
+            slot_extra.at[step],
+            held.at[SPLIT + step, :, pl.ds(0, TILE)],
+            extra_send.at[step],
+            slot_recv.at[step],
+            me + 3,
+        )
+
+    def extra_stat(step):
+        return remote(
+            stat_extra_out.at[step],
+            stat_extra_in.at[step],
+            extra_stat_send.at[step],
+            extra_stat_recv.at[step],
+            me + 2,
+        )
+
     def query_sent(head):
         return remote(
             query_held.at[head], query_held.at[head], query_send.at[head], query_send.at[head], me - 2
@@ -151,19 +183,13 @@
 
     @pl.when(has_prev)
     def _():
-        greet(me - 2)
-
-        @pl.when(even)
-        def _():
-            greet(me - 1)
+        greet(me - core - 2)
+        greet(me - core - 1)
 
     @pl.when(has_next)
     def _():
-        greet(me + 2)
-
-        @pl.when(odd)
-        def _():
-            greet(me + 1)
+        greet(me - core + 2)
+        greet(me - core + 3)
 
     @pl.loop(0, SPLIT)
     def _(step):
@@ -174,12 +200,12 @@
     lengths_load.start()
 
     @pl.loop(0, HK)
-    def _(head):
-        for copy in loads(head):
+    def _(turn):
+        for copy in loads(in_turn(turn)):
             copy.start()
 
-    back_peers = jnp.where(has_prev, 2 - core, 0)
-    next_peers = jnp.where(has_next, 1 + core, 0)
+    back_peers = jnp.where(has_prev, 2, 0)
+    next_peers = jnp.where(has_next, 2, 0)
     pl.semaphore_wait(barrier, 1 + back_peers + next_peers)
 
     @pl.loop(0, SPLIT)
@@ -190,17 +216,19 @@
         @pl.when(jnp.logical_and(even, has_prev))
         def _():
             for tile in range(tiles):
-                for side in range(2):
-                    query_to_prev(step, side, tile).start()
+                query_to_prev(step, 0, tile).start()
+                if tile == 0:
+                    extra_query(step).start()
+                else:
+                    query_to_prev(step, 1, tile).start()
 
     @pl.loop(0, HK)
-    def _(head):
+    def _(turn):
+        head = in_turn(turn)
         for copy in loads(head):
             copy.wait()
 
-        @pl.when(jnp.logical_or(even, head < SPLIT))
-        def _():
-            to_core(head).start()
+        to_core(head).start()
 
     @pl.when(jnp.logical_not(has_prev))
     def _():
@@ -209,8 +237,11 @@
         @pl.when(even)
         def _():
             stat_in[...] = jnp.full(stat_in.shape, MASKED, jnp.float32)
+            stat_extra_in[...] = jnp.full(stat_extra_in.shape, MASKED, jnp.float32)
 
     ones[...] = jnp.ones(ones.shape, ones.dtype)
+    stat_out[...] = jnp.full(stat_out.shape, MASKED, jnp.float32)
+    stat_extra_out[...] = jnp.full(stat_extra_out.shape, MASKED, jnp.float32)
 
     lengths_load.wait()
     doc_row = lax.broadcasted_iota(jnp.int32, (docs, docs), 0)
@@ -270,11 +301,12 @@
         both = jnp.dot(weights, values, preferred_element_type=jnp.float32).reshape(GROUPS, TILE, 2 * DH)
         return both[:, :, :DH], both[:, :, DH:]
 
-    def back_scores(step, head, tile):
+    def back_scores(step, head, tile, extra):
         begin = rows + tile * TILE
-        return raw_scores(query_back[step, pl.ds(tile * TILE, TILE), :], head, begin, 3 * rows - begin)
-
-    def back_finish(step, head, tile, raw):
+        queries = query_extra[step] if extra else query_back[step, pl.ds(tile * TILE, TILE), :]
+        return raw_scores(queries, head, begin, 3 * rows - begin)
+
+    def back_finish(step, head, tile, extra, raw):
         begin = rows + tile * TILE
         span = pl.ds(tile * TILE, TILE)
         scores = masked_scores(raw, back_bias[span, pl.ds(tile * TILE, 2 * rows - tile * TILE)])
@@ -285,9 +317,15 @@
         next_keys = as_float(next_begin) - mode[:1, :] <= rows
         for g in range(GROUPS):
             kept = held[head, g, pl.ds(2 * rows + tile * TILE, TILE), :].astype(jnp.float32)
-            slot[step, g, span, :] = jnp.where(next_keys, kept, mixed[g]).astype(jnp.bfloat16)
+            sent = jnp.where(next_keys, kept, mixed[g]).astype(jnp.bfloat16)
             row = jnp.sum(jnp.where(diagonal, level[g], 0.0), axis=0, keepdims=True)
-            stat_out[step, pl.ds(tile * GROUPS + g, 1), :] = jnp.where(next_keys, MASKED, row)
+            row = jnp.where(next_keys, MASKED, row)
+            if extra:
+                slot_extra[step, g] = sent
+                stat_extra_out[step, pl.ds(g, 1), :] = row
+            else:
+                slot[step, g, span, :] = sent
+                stat_out[step, pl.ds(tile * GROUPS + g, 1), :] = row
 
     def part_extent(side, tile):
         return rows, side * rows + (tile + 1) * TILE
@@ -310,41 +348,58 @@
         begin = side * tile * TILE
         return begin, rows - begin
 
-    def rest_scores(side, head, tile):
+    def rest_scores(side, head, step, tile):
         return raw_scores(query_held[head, pl.ds(tile * TILE, TILE), :], head, *rest_extent(side, tile))
 
-    def rest_finish(side, head, tile, raw):
+    def rest_finish(side, head, step, tile, raw):
         begin, count = rest_extent(side, tile)
         span = pl.ds(tile * TILE, TILE)
         scores = masked_scores(raw, bias[span, pl.ds(begin, count)])
-        before = part_high[head, :, span, :]
-        top = jnp.maximum(before, jnp.max(scores, axis=-1, keepdims=True))
-        if side == 0:
-            levels = []
-            for g in range(GROUPS):
-                row = stat_in[head, pl.ds(tile * GROUPS + g, 1), :]
-                levels.append(jnp.sum(jnp.where(diagonal, row, 0.0), axis=1, keepdims=True))
-            level = jnp.stack(levels)
-            top = jnp.maximum(top, level)
-        mixed, totals = weigh(scores, top[:, :, :1], head, begin)
-        scale = jnp.exp2(before - top)
-        mixed = mixed + part_mixed[head, :, span, :] * scale
-        totals = totals + part_total[head, :, span, :] * scale
-        if side == 0:
-            there = jnp.exp2(level - top)
-            mixed = mixed + held[head, :, span, :].astype(jnp.float32) * there
-            totals = totals + there
-        both = (mixed * (1.0 / totals)).astype(jnp.bfloat16)
+        tops, levels = [], []
         for g in range(GROUPS):
-            out_held[head, span, pl.ds(g * DH, DH)] = both[g]
-
-    def rest(side, head):
-        raw = rest_scores(side, head, 0)
-        for tile in range(tiles):
-            later = rest_scores(side, head, tile + 1) if tile + 1 < tiles else None
-            rest_finish(side, head, tile, raw)
+            top = jnp.maximum(part_high[head, g, span, :], jnp.max(scores[g], axis=-1, keepdims=True))
+            if side == 0:
+                if step is not None and tile == 0:
+                    row = stat_extra_in[step, pl.ds(g, 1), :]
+                else:
+                    row = stat_in[head, pl.ds(tile * GROUPS + g, 1), :]
+                level = jnp.sum(jnp.where(diagonal, row, 0.0), axis=1, keepdims=True)
+                top = jnp.maximum(top, level)
+                levels.append(level)
+            tops.append(top)
+        wide = jnp.stack([jnp.concatenate([top] * (count // DH), axis=1) for top in tops])
+        all_mixed, all_totals = weigh(scores, wide, head, begin)
+        for g in range(GROUPS):
+            scale = jnp.exp2(part_high[head, g, span, :] - tops[g])
+            mixed = all_mixed[g] + part_mixed[head, g, span, :] * scale
+            totals = all_totals[g] + part_total[head, g, span, :] * scale
+            if side == 0:
+                there = jnp.exp2(levels[g] - tops[g])
+                mixed = mixed + held[head, g, span, :].astype(jnp.float32) * there
+                totals = totals + there
+            out_ref[span, pl.ds(pl.multiple_of(head * WIDTH, WIDTH) + g * DH, DH)] = (mixed * (1.0 / totals)).astype(jnp.bfloat16)
+
+    def pipelined(jobs):
+        raw = jobs[0][0](*jobs[0][2])
+        for at, (_, finish, job) in enumerate(jobs):
+            later = None
+            if at + 1 < len(jobs):
+                later = jobs[at + 1][0](*jobs[at + 1][2])
+            finish(*job, raw)
             raw = later
-        out_store(head).start()
+
+    def back(side, step, tile):
+        return back_scores, back_finish, (step, side * SPLIT + step, tile, False)
+
+    def back_extra(step):
+        return back_scores, back_finish, (step, SPLIT + step, 0, True)
+
+    def part(side, head, tile):
+        return part_scores, part_finish, (side, head, tile)
+
+    def rest(side, step, at):
+        extra = step if at == 1 else None
+        pipelined([(rest_scores, rest_finish, (side, at * SPLIT + step, extra, tile)) for tile in range(tiles)])
 
     def wait_direct(side, step):
         @pl.when(has_prev)
@@ -360,49 +415,78 @@
             relay(step, 1 - side).wait_recv()
             if side == 0:
                 stat_to_next(step, SPLIT + step).wait_recv()
+                extra_stat(step).wait_recv()
+
+    def wait_query(side, step, tile):
+        @pl.when(has_next)
+        def _():
+            query_to_prev(step, 0, tile).wait_recv()
+            if side == 0 and tile == 1:
+                extra_query(step).wait_recv()
+
+    def send_slot(side, step, tile):
+        @pl.when(has_next)
+        def _():
+            slot_to_next(step, pl.ds(tile * TILE, TILE)).start()
+            if side == 0 and tile == 1:
+                extra_slot(step).start()
+                extra_stat(step).start()
+            if tile == tiles - 1:
+                stat_to_next(step, side * SPLIT + step).start()
 
     def run(side):
-        @pl.loop(0, HK if side else SPLIT)
-        def _(head):
-            from_core(head).wait_recv()
-
-        @pl.loop(0, SPLIT)
+        last = SPLIT - 1
+        first = side
+        from_core(0).wait_recv()
+        from_core(SPLIT).wait_recv()
+        pipelined([part(side, head, tile) for head in (0, SPLIT) for tile in range(tiles)])
+
+        def backs(step, tile):
+            jobs = [back(side, step, tile)]
+            return [back_extra(step)] + jobs if side == 0 and tile == 1 else jobs
+
+        @pl.loop(0, last)
         def _(step):
-            head = side * SPLIT + step
-            for tile in range(tiles):
-                @pl.when(has_next)
-                def _():
-                    query_to_prev(step, 0, tile).wait_recv()
-
-                raw_back = back_scores(step, head, tile)
-                raw_first = part_scores(side, step, tile)
-                back_finish(step, head, tile, raw_back)
-
-                @pl.when(has_next)
-                def _():
-                    slot_to_next(step, pl.ds(tile * TILE, TILE)).start()
-                    if tile == tiles - 1:
-                        stat_to_next(step, head).start()
-
-                raw_second = part_scores(side, SPLIT + step, tile)
-                part_finish(side, step, tile, raw_first)
-                part_finish(side, SPLIT + step, tile, raw_second)
-
-                if tile == tiles - 2:
-                    @pl.when(step >= 1)
+            from_core(step + 1).wait_recv()
+            from_core(SPLIT + step + 1).wait_recv()
+            for tile in range(first, tiles):
+                wait_query(side, step, tile)
+                jobs = backs(step, tile)
+                for at in range(0 if tile == first else tile, tile + 1):
+                    jobs.append(part(side, step + 1, at))
+                    jobs.append(part(side, SPLIT + step + 1, at))
+                pipelined(jobs)
+                send_slot(side, step, tile)
+                if tile == first:
+
+                    @pl.when(step >= 2)
                     def _():
-                        wait_direct(side, step - 1)
-
-            @pl.when(step >= 1)
+                        wait_direct(side, step - 2)
+
+            @pl.when(step >= 2)
             def _():
-                rest(side, side * SPLIT + step - 1)
-                wait_relayed(side, step - 1)
-                rest(side, (1 - side) * SPLIT + step - 1)
-
-        wait_direct(side, SPLIT - 1)
-        rest(side, side * SPLIT + SPLIT - 1)
-        wait_relayed(side, SPLIT - 1)
-        rest(side, (1 - side) * SPLIT + SPLIT - 1)
+                rest(side, step - 2, side)
+                wait_relayed(side, step - 2)
+                rest(side, step - 2, 1 - side)
+
+        for tile in range(first, tiles):
+            wait_query(side, last, tile)
+            pipelined(backs(last, tile))
+            send_slot(side, last, tile)
+            if tile == first:
+                wait_direct(side, last - 2)
+
+        wait_direct(side, last - 1)
+        rest(side, last - 2, side)
+        wait_relayed(side, last - 2)
+        rest(side, last - 2, 1 - side)
+        rest(side, last - 1, side)
+        wait_relayed(side, last - 1)
+        rest(side, last - 1, 1 - side)
+        wait_direct(side, last)
+        rest(side, last, side)
+        wait_relayed(side, last)
+        rest(side, last, 1 - side)
 
     @pl.when(even)
     def _():
@@ -414,18 +498,23 @@
 
     @pl.loop(0, HK)
     def _(head):
-        out_store(head).wait()
-
-        @pl.when(jnp.logical_or(even, head < SPLIT))
-        def _():
-            to_core(head).wait_send()
+        to_core(head).wait_send()
 
     @pl.loop(0, SPLIT)
     def _(step):
         @pl.when(has_next)
         def _():
-            slot_to_next(step, received).wait_send()
             stat_to_next(step, step).wait_send()
+
+            @pl.when(even)
+            def _():
+                slot_to_next(step, received).wait_send()
+                extra_slot(step).wait_send()
+                extra_stat(step).wait_send()
+
+            @pl.when(odd)
+            def _():
+                slot_to_next(step, pl.ds(TILE, rows - TILE)).wait_send()
 
         @pl.when(has_prev)
         def _():
@@ -443,20 +532,23 @@
     shards = lax.axis_size("cp")
     stats = rows // TILE * GROUPS
     dma = pltpu.SemaphoreType.DMA
-    hbm = pl.BlockSpec(memory_space=pl.ANY)
+    hbm = pl.BlockSpec(memory_space=pltpu.HBM)
     return pl.pallas_call(
         functools.partial(kernel, shards),
-        out_shape=jax.ShapeDtypeStruct(queries.shape, queries.dtype),
+        out_shape=pltpu.VMEM(queries.shape, queries.dtype),
         in_specs=[hbm] * 4,
-        out_specs=hbm,
+        out_specs=pl.BlockSpec(memory_space=pltpu.VMEM),
         scratch_shapes=[
             pltpu.VMEM((HK, 2, 3 * rows, DH), keys.dtype),
             pltpu.VMEM((HK, rows, WIDTH), queries.dtype),
-            pltpu.VMEM((HK, rows, WIDTH), queries.dtype),
             pltpu.VMEM((SPLIT, rows, WIDTH), queries.dtype),
+            pltpu.VMEM((SPLIT, TILE, WIDTH), queries.dtype),
             pltpu.VMEM((SPLIT, 2, rows, DH), keys.dtype),
+            pltpu.VMEM((SPLIT, 2, TILE, DH), keys.dtype),
             pltpu.VMEM((SPLIT, stats, TILE), jnp.float32),
             pltpu.VMEM((HK, stats, TILE), jnp.float32),
+            pltpu.VMEM((SPLIT, 8, TILE), jnp.float32),
+            pltpu.VMEM((SPLIT, 8, TILE), jnp.float32),
             pltpu.VMEM((rows, 3 * rows), jnp.float32),
             pltpu.VMEM((rows, 2 * rows), jnp.float32),
             pltpu.VMEM((1, docs), jnp.int32),
@@ -471,8 +563,11 @@
             dma((HK,)),
             dma((HK,)),
             dma((HK,)),
-            dma((HK,)),
             dma((SPLIT, rows // TILE)),
+            dma((SPLIT,)),
+            dma((SPLIT,)),
+            dma((SPLIT,)),
+            dma((SPLIT,)),
             dma((SPLIT,)),
             dma((SPLIT,)),
             dma((SPLIT,)),
@@ -481,9 +576,9 @@
             dma((HK,)),
         ],
         compiler_params=pltpu.CompilerParams(
-            collective_id=0, has_side_effects=True, vmem_limit_bytes=58 * 1024 * 1024
+            collective_id=0, has_side_effects=True, vmem_limit_bytes=50 * 1024 * 1024
         ),
-    )(doc_lengths.reshape(1, docs), queries, keys, values)
+    )(*(pltpu.with_memory_space_constraint(x, pltpu.HBM) for x in (doc_lengths.reshape(1, docs), queries, keys, values)))
 
 
 def solution(mesh):

time: 46.6 us -> 38 us (0.82)
  the two profiles are of different devices: /device:TPU:1 before, /device:TPU:0 now
where the time goes in v2:
time: 38 us; the launch traced here: 37.7 us
  Pallas kernels  36.4 us (96%)
  local copies, waits for them, and re-layouts  1.32 us (3%)
    pallas_call x1, Pallas kernels, on_device(): pl.pallas_call(functools.partial(kernel, shards), out_shape=pltpu.VMEM(qu...  36.4 us
    unnamed x1, local copies, waits for them, and re-layouts  1.32 us

profile of v2, /device:TPU:0, one launch (start us, length us, event | category | flops | bytes accessed | tf_op | source)
XLA Modules:
  0.0 37.7 jit_solution(2408349189173176843)
XLA Ops:
  0.0 36.4 %shard_map.46 = bf16[512,2048]{1,0:T(8,128)(2,1)S(1)} custom-call(s32[1,32]{1,0:T(1,128)} %bitcast.1, bf16[512,2048]{1,0:T(8,128)(2,1)} %queries_ref.1, bf16[512,1024]{1,0:T(8,128)(2,1)} %keys_ref.1, bf16[512,1024]{1,0:T(8,128)(2,1)} %values_ref.1), custom_call_target="tpu_custom_call" | custom-call | tf_op jit(solution)/shard_map/pallas_call | solution.py:536
  36.4 1.3 %copy.6 = bf16[512,2048]{1,0:T(8,128)(2,1)} copy(bf16[512,2048]{1,0:T(8,128)(2,1)S(1)} %shard_map.46) | data formatting | bytes 4194304

commit v3 on v2

--- a/solution.py
+++ b/solution.py
@@ -17,6 +17,7 @@
 STACK = GROUPS * TILE
 MASKED = -1e30
 SPLIT = HK // 2
+FORWARD = HK - 1
 MESH = pl.DeviceIdType.MESH
 
 LOG2E = math.log2(math.e)
@@ -33,15 +34,13 @@
     held,
     query_held,
     query_back,
-    query_extra,
+    far_held,
     slot,
-    slot_extra,
     stat_out,
     stat_in,
-    stat_extra_out,
-    stat_extra_in,
     bias,
     back_bias,
+    far_bias,
     lengths,
     mode,
     ones,
@@ -49,16 +48,14 @@
     part_total,
     part_high,
     lengths_sem,
+    far_send,
+    far_recv,
     load_sem,
     query_sem,
     core_send,
     core_recv,
     query_send,
     query_recv,
-    extra_recv,
-    extra_send,
-    extra_stat_send,
-    extra_stat_recv,
     slot_send,
     slot_recv,
     relay_send,
@@ -89,7 +86,8 @@
         )
 
     def in_turn(turn):
-        return lax.rem(turn, 2) * SPLIT + turn // 2
+        order = lax.rem(turn + HK - 1, HK)
+        return lax.rem(order, 2) * SPLIT + order // 2
 
     def query_load(head):
         lanes = pl.ds(pl.multiple_of(head * WIDTH, WIDTH), WIDTH)
@@ -122,30 +120,15 @@
             me - 2 + side,
         )
 
-    def extra_query(step):
+    def far_to_next():
+        return remote(held.at[FORWARD, :, own], far_held, far_send, far_recv, me + 2)
+
+    def near_to_next():
         return remote(
-            query_held.at[SPLIT + step, pl.ds(0, TILE)],
-            query_extra.at[step],
-            query_send.at[SPLIT + step],
-            extra_recv.at[step],
-            me - 2,
-        )
-
-    def extra_slot(step):
-        return remote(
-            slot_extra.at[step],
-            held.at[SPLIT + step, :, pl.ds(0, TILE)],
-            extra_send.at[step],
-            slot_recv.at[step],
-            me + 3,
-        )
-
-    def extra_stat(step):
-        return remote(
-            stat_extra_out.at[step],
-            stat_extra_in.at[step],
-            extra_stat_send.at[step],
-            extra_stat_recv.at[step],
+            held.at[FORWARD, :, own],
+            held.at[FORWARD, :, received],
+            slot_send.at[SPLIT - 1],
+            slot_recv.at[SPLIT - 1],
             me + 2,
         )
 
@@ -154,19 +137,22 @@
             query_held.at[head], query_held.at[head], query_send.at[head], query_send.at[head], me - 2
         )
 
-    def slot_to_next(step, span):
+    def arrival(step, tile):
+        return step + tile if step is SPLIT - 1 else step
+
+    def slot_to_next(step, span, tile=0):
         return remote(
             slot.at[step, :, span],
             held.at[core * SPLIT + step, :, span],
             slot_send.at[step],
-            slot_recv.at[step],
+            slot_recv.at[arrival(step, tile)],
             me + 2,
         )
 
-    def relay(step, side):
+    def relay(step, side, span=received):
         head = side * SPLIT + step
         return remote(
-            held.at[head, :, received], held.at[head, :, received], relay_send.at[step], relay_recv.at[step], partner
+            held.at[head, :, span], held.at[head, :, span], relay_send.at[step], relay_recv.at[step], partner
         )
 
     def stat_to_next(step, head):
@@ -217,9 +203,9 @@
         def _():
             for tile in range(tiles):
                 query_to_prev(step, 0, tile).start()
-                if tile == 0:
-                    extra_query(step).start()
-                else:
+
+                @pl.when(step < SPLIT - 1)
+                def _():
                     query_to_prev(step, 1, tile).start()
 
     @pl.loop(0, HK)
@@ -228,6 +214,16 @@
         for copy in loads(head):
             copy.wait()
 
+        @pl.when(jnp.logical_and(has_next, turn == 0))
+        def _():
+            @pl.when(even)
+            def _():
+                far_to_next().start()
+
+            @pl.when(odd)
+            def _():
+                near_to_next().start()
+
         to_core(head).start()
 
     @pl.when(jnp.logical_not(has_prev))
@@ -236,12 +232,11 @@
 
         @pl.when(even)
         def _():
+            far_held[...] = jnp.zeros(far_held.shape, far_held.dtype)
             stat_in[...] = jnp.full(stat_in.shape, MASKED, jnp.float32)
-            stat_extra_in[...] = jnp.full(stat_extra_in.shape, MASKED, jnp.float32)
 
     ones[...] = jnp.ones(ones.shape, ones.dtype)
     stat_out[...] = jnp.full(stat_out.shape, MASKED, jnp.float32)
-    stat_extra_out[...] = jnp.full(stat_extra_out.shape, MASKED, jnp.float32)
 
     lengths_load.wait()
     doc_row = lax.broadcasted_iota(jnp.int32, (docs, docs), 0)
@@ -273,7 +268,10 @@
     floor = jnp.where(here - begin_here <= rows, 0.0, here)
     for tile in range(tiles):
         query_pos = (me * rows + tile * TILE + row_iota).astype(jnp.float32)
-        begins = jnp.maximum(doc_begins(query_pos), floor)
+        begins = doc_begins(query_pos)
+        far_pos = (chip_begin - 2 * rows + lax.broadcasted_iota(jnp.int32, (TILE, 2 * rows), 1)).astype(jnp.float32)
+        far_bias[pl.ds(tile * TILE, TILE), :] = jnp.where(far_pos >= begins, 0.0, MASKED)
+        begins = jnp.maximum(begins, floor)
         key_pos = (chip_begin - rows + lax.broadcasted_iota(jnp.int32, (TILE, 3 * rows), 1)).astype(jnp.float32)
         visible = (key_pos >= begins) & (key_pos <= query_pos)
         bias[pl.ds(tile * TILE, TILE), :] = jnp.where(visible, 0.0, MASKED)
@@ -285,28 +283,32 @@
     def stack(queries):
         return jnp.concatenate([queries[:, g * DH : (g + 1) * DH] for g in range(GROUPS)], axis=0)
 
-    def raw_scores(queries, head, begin, count):
-        keys = held[head, 0, pl.ds(begin, count), :]
+    def dot_keys(queries, keys):
         return lax.dot_general(
             stack(queries), keys, (((1,), (1,)), ((), ())), preferred_element_type=jnp.float32
         )
 
+    def raw_scores(queries, head, begin, count):
+        return dot_keys(queries, held[head, 0, pl.ds(begin, count), :])
+
     def masked_scores(raw, mask):
         return raw.reshape(GROUPS, TILE, raw.shape[-1]) * exponent_scale + mask[None]
 
     def weigh(scores, highest, head, begin):
+        return mix(scores, highest, held[head, 1, pl.ds(begin, scores.shape[-1]), :])
+
+    def mix(scores, highest, values):
         count = scores.shape[-1]
         weights = jnp.exp2(scores - highest).astype(jnp.bfloat16).reshape(STACK, count)
-        values = jnp.concatenate([held[head, 1, pl.ds(begin, count), :], ones[pl.ds(0, count), :]], axis=1)
+        values = jnp.concatenate([values, ones[pl.ds(0, count), :]], axis=1)
         both = jnp.dot(weights, values, preferred_element_type=jnp.float32).reshape(GROUPS, TILE, 2 * DH)
         return both[:, :, :DH], both[:, :, DH:]
 
-    def back_scores(step, head, tile, extra):
+    def back_scores(step, head, tile):
         begin = rows + tile * TILE
-        queries = query_extra[step] if extra else query_back[step, pl.ds(tile * TILE, TILE), :]
-        return raw_scores(queries, head, begin, 3 * rows - begin)
-
-    def back_finish(step, head, tile, extra, raw):
+        return raw_scores(query_back[step, pl.ds(tile * TILE, TILE), :], head, begin, 3 * rows - begin)
+
+    def back_finish(step, head, tile, raw):
         begin = rows + tile * TILE
         span = pl.ds(tile * TILE, TILE)
         scores = masked_scores(raw, back_bias[span, pl.ds(tile * TILE, 2 * rows - tile * TILE)])
@@ -320,12 +322,8 @@
             sent = jnp.where(next_keys, kept, mixed[g]).astype(jnp.bfloat16)
             row = jnp.sum(jnp.where(diagonal, level[g], 0.0), axis=0, keepdims=True)
             row = jnp.where(next_keys, MASKED, row)
-            if extra:
-                slot_extra[step, g] = sent
-                stat_extra_out[step, pl.ds(g, 1), :] = row
-            else:
-                slot[step, g, span, :] = sent
-                stat_out[step, pl.ds(tile * GROUPS + g, 1), :] = row
+            slot[step, g, span, :] = sent
+            stat_out[step, pl.ds(tile * GROUPS + g, 1), :] = row
 
     def part_extent(side, tile):
         return rows, side * rows + (tile + 1) * TILE
@@ -348,36 +346,52 @@
         begin = side * tile * TILE
         return begin, rows - begin
 
-    def rest_scores(side, head, step, tile):
+    def rest_scores(side, head, tile):
         return raw_scores(query_held[head, pl.ds(tile * TILE, TILE), :], head, *rest_extent(side, tile))
 
-    def rest_finish(side, head, step, tile, raw):
+    def rest_finish(side, head, tile, raw):
         begin, count = rest_extent(side, tile)
+        mask = bias[pl.ds(tile * TILE, TILE), pl.ds(begin, count)]
+        rows_of = []
+        if side == 0:
+            for g in range(GROUPS):
+                rows_of.append(stat_in[head, pl.ds(tile * GROUPS + g, 1), :])
+        merge(head, tile, masked_scores(raw, mask), held[head, 1, pl.ds(begin, count), :], rows_of)
+
+    def far_scores(tile):
+        begin = tile * TILE
+        keys = jnp.concatenate([far_held[0, pl.ds(begin, rows - begin), :], held[FORWARD, 0, received, :]], axis=0)
+        return dot_keys(query_held[FORWARD, pl.ds(begin, TILE), :], keys)
+
+    def far_finish(tile, raw):
+        begin = tile * TILE
+        mask = far_bias[pl.ds(begin, TILE), pl.ds(begin, 2 * rows - begin)]
+        values = jnp.concatenate([far_held[1, pl.ds(begin, rows - begin), :], held[FORWARD, 1, received, :]], axis=0)
+        merge(FORWARD, tile, masked_scores(raw, mask), values, [])
+
+    def merge(head, tile, scores, values, level_rows):
         span = pl.ds(tile * TILE, TILE)
-        scores = masked_scores(raw, bias[span, pl.ds(begin, count)])
         tops, levels = [], []
         for g in range(GROUPS):
             top = jnp.maximum(part_high[head, g, span, :], jnp.max(scores[g], axis=-1, keepdims=True))
-            if side == 0:
-                if step is not None and tile == 0:
-                    row = stat_extra_in[step, pl.ds(g, 1), :]
-                else:
-                    row = stat_in[head, pl.ds(tile * GROUPS + g, 1), :]
-                level = jnp.sum(jnp.where(diagonal, row, 0.0), axis=1, keepdims=True)
+            if level_rows:
+                level = jnp.sum(jnp.where(diagonal, level_rows[g], 0.0), axis=1, keepdims=True)
                 top = jnp.maximum(top, level)
                 levels.append(level)
             tops.append(top)
-        wide = jnp.stack([jnp.concatenate([top] * (count // DH), axis=1) for top in tops])
-        all_mixed, all_totals = weigh(scores, wide, head, begin)
+        wide = jnp.stack([jnp.concatenate([top] * (scores.shape[-1] // DH), axis=1) for top in tops])
+        all_mixed, all_totals = mix(scores, wide, values)
         for g in range(GROUPS):
             scale = jnp.exp2(part_high[head, g, span, :] - tops[g])
             mixed = all_mixed[g] + part_mixed[head, g, span, :] * scale
             totals = all_totals[g] + part_total[head, g, span, :] * scale
-            if side == 0:
+            if level_rows:
                 there = jnp.exp2(levels[g] - tops[g])
                 mixed = mixed + held[head, g, span, :].astype(jnp.float32) * there
                 totals = totals + there
-            out_ref[span, pl.ds(pl.multiple_of(head * WIDTH, WIDTH) + g * DH, DH)] = (mixed * (1.0 / totals)).astype(jnp.bfloat16)
+            out_ref[span, pl.ds(pl.multiple_of(head * WIDTH, WIDTH) + g * DH, DH)] = (
+                mixed * (1.0 / totals)
+            ).astype(jnp.bfloat16)
 
     def pipelined(jobs):
         raw = jobs[0][0](*jobs[0][2])
@@ -389,25 +403,45 @@
             raw = later
 
     def back(side, step, tile):
-        return back_scores, back_finish, (step, side * SPLIT + step, tile, False)
-
-    def back_extra(step):
-        return back_scores, back_finish, (step, SPLIT + step, 0, True)
+        return back_scores, back_finish, (step, side * SPLIT + step, tile)
 
     def part(side, head, tile):
         return part_scores, part_finish, (side, head, tile)
 
+    def rest_jobs(side, step, at):
+        return [(rest_scores, rest_finish, (side, at * SPLIT + step, tile)) for tile in range(tiles)]
+
     def rest(side, step, at):
-        extra = step if at == 1 else None
-        pipelined([(rest_scores, rest_finish, (side, at * SPLIT + step, extra, tile)) for tile in range(tiles)])
+        pipelined(rest_jobs(side, step, at))
+
+    def rest_far():
+        pipelined([(far_scores, far_finish, (tile,)) for tile in range(tiles)])
 
     def wait_direct(side, step):
         @pl.when(has_prev)
         def _():
-            slot_to_next(step, received).wait_recv()
-            relay(step, side).start()
+            if step is SPLIT - 1:
+                for tile in range(tiles):
+                    span = pl.ds(tile * TILE, TILE)
+                    slot_to_next(step, span, tile).wait_recv()
+                    relay(step, side, span).start()
+            else:
+                slot_to_next(step, received).wait_recv()
+                relay(step, side).start()
             if side == 0:
                 stat_to_next(step, step).wait_recv()
+
+    def wait_near():
+        @pl.when(has_prev)
+        def _():
+            near_to_next().wait_recv()
+            relay(SPLIT - 1, 1).start()
+
+    def wait_far():
+        @pl.when(has_prev)
+        def _():
+            far_to_next().wait_recv()
+            relay(SPLIT - 1, 1).wait_recv()
 
     def wait_relayed(side, step):
         @pl.when(has_prev)
@@ -415,35 +449,32 @@
             relay(step, 1 - side).wait_recv()
             if side == 0:
                 stat_to_next(step, SPLIT + step).wait_recv()
-                extra_stat(step).wait_recv()
 
     def wait_query(side, step, tile):
         @pl.when(has_next)
         def _():
             query_to_prev(step, 0, tile).wait_recv()
-            if side == 0 and tile == 1:
-                extra_query(step).wait_recv()
 
     def send_slot(side, step, tile):
         @pl.when(has_next)
         def _():
-            slot_to_next(step, pl.ds(tile * TILE, TILE)).start()
-            if side == 0 and tile == 1:
-                extra_slot(step).start()
-                extra_stat(step).start()
+            slot_to_next(step, pl.ds(tile * TILE, TILE), tile).start()
             if tile == tiles - 1:
                 stat_to_next(step, side * SPLIT + step).start()
 
     def run(side):
         last = SPLIT - 1
-        first = side
-        from_core(0).wait_recv()
-        from_core(SPLIT).wait_recv()
+        first = 0
+        if side == 1:
+            from_core(0).wait_recv()
+            from_core(SPLIT).wait_recv()
         pipelined([part(side, head, tile) for head in (0, SPLIT) for tile in range(tiles)])
+        if side == 0:
+            from_core(0).wait_recv()
+            from_core(SPLIT).wait_recv()
 
         def backs(step, tile):
-            jobs = [back(side, step, tile)]
-            return [back_extra(step)] + jobs if side == 0 and tile == 1 else jobs
+            return [back(side, step, tile)]
 
         @pl.loop(0, last)
         def _(step):
@@ -462,6 +493,8 @@
                     @pl.when(step >= 2)
                     def _():
                         wait_direct(side, step - 2)
+                        if side == 1:
+                            wait_near()
 
             @pl.when(step >= 2)
             def _():
@@ -469,24 +502,41 @@
                 wait_relayed(side, step - 2)
                 rest(side, step - 2, 1 - side)
 
-        for tile in range(first, tiles):
-            wait_query(side, last, tile)
-            pipelined(backs(last, tile))
-            send_slot(side, last, tile)
-            if tile == first:
-                wait_direct(side, last - 2)
-
-        wait_direct(side, last - 1)
-        rest(side, last - 2, side)
-        wait_relayed(side, last - 2)
-        rest(side, last - 2, 1 - side)
-        rest(side, last - 1, side)
-        wait_relayed(side, last - 1)
-        rest(side, last - 1, 1 - side)
-        wait_direct(side, last)
-        rest(side, last, side)
-        wait_relayed(side, last)
-        rest(side, last, 1 - side)
+        if side == 0:
+            for tile in range(tiles):
+                wait_query(side, last, tile)
+                jobs = backs(last, tile)
+                if tile == 1:
+                    jobs += rest_jobs(side, last - 2, 0)
+                if tile == 3:
+                    jobs += rest_jobs(side, last - 2, 1)
+                pipelined(jobs)
+                send_slot(side, last, tile)
+                if tile == 0:
+                    wait_direct(side, last - 2)
+                if tile == 2:
+                    wait_relayed(side, last - 2)
+                    wait_direct(side, last - 1)
+
+            wait_far()
+            rest_far()
+            rest(side, last - 1, 0)
+            wait_relayed(side, last - 1)
+            rest(side, last - 1, 1)
+            wait_direct(side, last)
+            rest(side, last, 0)
+        else:
+            wait_direct(side, last - 2)
+            rest(side, last, 1)
+            rest(side, last - 2, 1)
+            wait_relayed(side, last - 2)
+            wait_direct(side, last - 1)
+            rest(side, last - 2, 0)
+            rest(side, last - 1, 1)
+            wait_relayed(side, last - 1)
+            rest(side, last - 1, 0)
+            wait_relayed(side, last)
+            rest(side, last, 0)
 
     @pl.when(even)
     def _():
@@ -500,30 +550,37 @@
     def _(head):
         to_core(head).wait_send()
 
-    @pl.loop(0, SPLIT)
-    def _(step):
-        @pl.when(has_next)
-        def _():
-            stat_to_next(step, step).wait_send()
+    @pl.when(has_next)
+    def _():
+        @pl.when(even)
+        def _():
+            far_to_next().wait_send()
+
+        @pl.when(odd)
+        def _():
+            near_to_next().wait_send()
+
+        for step in range(SPLIT):
 
             @pl.when(even)
             def _():
                 slot_to_next(step, received).wait_send()
-                extra_slot(step).wait_send()
-                extra_stat(step).wait_send()
-
-            @pl.when(odd)
+                stat_to_next(step, step).wait_send()
+
+            @pl.when(jnp.logical_and(odd, step < SPLIT - 1))
             def _():
-                slot_to_next(step, pl.ds(TILE, rows - TILE)).wait_send()
-
-        @pl.when(has_prev)
-        def _():
+                slot_to_next(step, received).wait_send()
+                stat_to_next(step, step).wait_send()
+
+    @pl.when(has_prev)
+    def _():
+        for step in range(SPLIT):
             relay(step, core).wait_send()
 
-            @pl.when(even)
-            def _():
-                for side in range(2):
-                    query_sent(side * SPLIT + step).wait_send()
+        @pl.when(even)
+        def _():
+            for head in range(HK - 1):
+                query_sent(head).wait_send()
 
 
 def on_device(queries, keys, values, doc_lengths):
@@ -542,14 +599,12 @@
             pltpu.VMEM((HK, 2, 3 * rows, DH), keys.dtype),
             pltpu.VMEM((HK, rows, WIDTH), queries.dtype),
             pltpu.VMEM((SPLIT, rows, WIDTH), queries.dtype),
-            pltpu.VMEM((SPLIT, TILE, WIDTH), queries.dtype),
+            pltpu.VMEM((2, rows, DH), keys.dtype),
             pltpu.VMEM((SPLIT, 2, rows, DH), keys.dtype),
-            pltpu.VMEM((SPLIT, 2, TILE, DH), keys.dtype),
             pltpu.VMEM((SPLIT, stats, TILE), jnp.float32),
             pltpu.VMEM((HK, stats, TILE), jnp.float32),
-            pltpu.VMEM((SPLIT, 8, TILE), jnp.float32),
-            pltpu.VMEM((SPLIT, 8, TILE), jnp.float32),
             pltpu.VMEM((rows, 3 * rows), jnp.float32),
+            pltpu.VMEM((rows, 2 * rows), jnp.float32),
             pltpu.VMEM((rows, 2 * rows), jnp.float32),
             pltpu.VMEM((1, docs), jnp.int32),
             pltpu.VMEM((8, DH), jnp.float32),
@@ -558,6 +613,8 @@
             pltpu.VMEM((HK, GROUPS, rows, DH), jnp.float32),
             pltpu.VMEM((HK, GROUPS, rows, DH), jnp.float32),
             dma,
+            dma,
+            dma,
             dma((HK, 2)),
             dma((HK,)),
             dma((HK,)),
@@ -565,11 +622,7 @@
             dma((HK,)),
             dma((SPLIT, rows // TILE)),
             dma((SPLIT,)),
-            dma((SPLIT,)),
-            dma((SPLIT,)),
-            dma((SPLIT,)),
-            dma((SPLIT,)),
-            dma((SPLIT,)),
+            dma((SPLIT + rows // TILE - 1,)),
             dma((SPLIT,)),
             dma((SPLIT,)),
             dma((SPLIT,)),

time: 38 us -> 37.3 us (0.982)
  Pallas kernels: 36.4 us -> 35.8 us
    pallas_call x1, Pallas kernels: 36.4 us -> 35.8 us  [on_device(): pl.pallas_call(functools.partial(kernel, shards), out_shape=pltpu.VMEM(qu...]
where the time goes in v3:
time: 37.3 us; the launch traced here: 37.1 us
  Pallas kernels  35.8 us (96%)
  local copies, waits for them, and re-layouts  1.32 us (4%)
    pallas_call x1, Pallas kernels, on_device(): pl.pallas_call(functools.partial(kernel, shards), out_shape=pltpu.VMEM(qu...  35.8 us
    unnamed x1, local copies, waits for them, and re-layouts  1.32 us

profile of v3, /device:TPU:0, one launch (start us, length us, event | category | flops | bytes accessed | tf_op | source)
XLA Modules:
  0.0 37.1 jit_solution(8271119501439135191)
XLA Ops:
  0.0 35.8 %shard_map.46 = bf16[512,2048]{1,0:T(8,128)(2,1)S(1)} custom-call(s32[1,32]{1,0:T(1,128)} %bitcast.1, bf16[512,2048]{1,0:T(8,128)(2,1)} %queries_ref.1, bf16[512,1024]{1,0:T(8,128)(2,1)} %keys_ref.1, bf16[512,1024]{1,0:T(8,128)(2,1)} %values_ref.1), custom_call_target="tpu_custom_call" | custom-call | tf_op jit(solution)/shard_map/pallas_call | solution.py:593
  35.8 1.3 %copy.6 = bf16[512,2048]{1,0:T(8,128)(2,1)} copy(bf16[512,2048]{1,0:T(8,128)(2,1)S(1)} %shard_map.46) | data formatting | bytes 4194304

commit v4 on v3

--- a/solution.py
+++ b/solution.py
@@ -414,8 +414,8 @@
     def rest(side, step, at):
         pipelined(rest_jobs(side, step, at))
 
-    def rest_far():
-        pipelined([(far_scores, far_finish, (tile,)) for tile in range(tiles)])
+    def far_jobs():
+        return [(far_scores, far_finish, (tile,)) for tile in range(tiles)]
 
     def wait_direct(side, step):
         @pl.when(has_prev)
@@ -518,21 +518,17 @@
                     wait_relayed(side, last - 2)
                     wait_direct(side, last - 1)
 
+            wait_relayed(side, last - 1)
+            pipelined(rest_jobs(side, last - 1, 0) + rest_jobs(side, last - 1, 1))
+            wait_direct(side, last)
             wait_far()
-            rest_far()
-            rest(side, last - 1, 0)
-            wait_relayed(side, last - 1)
-            rest(side, last - 1, 1)
-            wait_direct(side, last)
-            rest(side, last, 0)
+            pipelined(far_jobs() + rest_jobs(side, last, 0))
         else:
             wait_direct(side, last - 2)
-            rest(side, last, 1)
-            rest(side, last - 2, 1)
+            pipelined(rest_jobs(side, last, 1) + rest_jobs(side, last - 2, 1))
             wait_relayed(side, last - 2)
             wait_direct(side, last - 1)
-            rest(side, last - 2, 0)
-            rest(side, last - 1, 1)
+            pipelined(rest_jobs(side, last - 2, 0) + rest_jobs(side, last - 1, 1))
             wait_relayed(side, last - 1)
             rest(side, last - 1, 0)
             wait_relayed(side, last)

time: 37.3 us -> 37 us (level)
  no operation moved by 1% of the time
where the time goes in v4:
time: 37 us; the launch traced here: 36.8 us
  Pallas kernels  35.5 us (96%)
  local copies, waits for them, and re-layouts  1.32 us (4%)
    pallas_call x1, Pallas kernels, on_device(): pl.pallas_call(functools.partial(kernel, shards), out_shape=pltpu.VMEM(qu...  35.5 us
    unnamed x1, local copies, waits for them, and re-layouts  1.32 us

profile of v4, /device:TPU:0, one launch (start us, length us, event | category | flops | bytes accessed | tf_op | source)
XLA Modules:
  0.0 36.8 jit_solution(8451984259996200333)
XLA Ops:
  0.0 35.5 %shard_map.46 = bf16[512,2048]{1,0:T(8,128)(2,1)S(1)} custom-call(s32[1,32]{1,0:T(1,128)} %bitcast.1, bf16[512,2048]{1,0:T(8,128)(2,1)} %queries_ref.1, bf16[512,1024]{1,0:T(8,128)(2,1)} %keys_ref.1, bf16[512,1024]{1,0:T(8,128)(2,1)} %values_ref.1), custom_call_target="tpu_custom_call" | custom-call | tf_op jit(solution)/shard_map/pallas_call | solution.py:589
  35.5 1.3 %copy.6 = bf16[512,2048]{1,0:T(8,128)(2,1)} copy(bf16[512,2048]{1,0:T(8,128)(2,1)S(1)} %shard_map.46) | data formatting | bytes 4194304
